TPU v7x, 256 devices: a whole 4x4x8 slice. The times are simulated.
256 devices in a mesh: ep: 64 (over x, z, core), dp: 4 (over y).
Axes of the slice: x: 4, y: 4, z: 8, core: 2. Of those that a mesh axis runs over, the one named last changes fastest.
Arguments:
- tokens: bfloat16 [32768, 2048], P(('ep', 'dp')), may hold values from -6 to 6
- routes: int32 [32768, 8], P(('ep', 'dp')), may hold values from 0 to 63, as said below
- gates: bfloat16 [32768, 8], P(('ep', 'dp')), may hold values from 0.19921875 to 1
- w_gate: bfloat16 [64, 2048, 768], P('ep'), may hold values from -0.125 to 0.125
- w_up: bfloat16 [64, 2048, 768], P('ep'), may hold values from -0.125 to 0.125
- w_down: bfloat16 [64, 768, 2048], P('ep'), may hold values from -0.21875 to 0.21875
- score_head: float32 [2048], replicated, may hold values from -0.125 to 0.125
- doc_ids: int32 [256], P(('ep', 'dp')), may hold values from 0 to 63, never falling along the last dimension, each value on 1 to 8 neighbouring positions
Outputs:
- mixed: bfloat16 [32768, 2048], P(('ep', 'dp'))
- doc_scores: float32 [3, 64], replicated
Inputs may be any that keep to these rules, and one draw needn't show every extreme that they name: `routes`: each row names 8 different experts; among the rows of one device no expert is named more than 24 times. `doc_ids`: never falling along the passages; every document has 1 to 8 passages.
All inputs are finite; a program needn't handle non-finite values.
Results may differ from a plain program's by a relative error of at most 0.0058.
Values may be sent and summed in bfloat16 or wider, within the bound.
A program may use at most 64 MiB of HBM per device.

v0:
```python
import math
import jax
import jax.numpy as jnp
from jax import lax
from jax.sharding import Mesh
from jax.sharding import PartitionSpec as P

TOP = 8
PASSAGE = 128
EP = ("x", "z", "core")
EP_DP = ("x", "z", "core", "dp")
CAP = 24


def shards(tokens, routes, gates, w_gate, w_up, w_down, score_head, doc_ids):
    rows, width = tokens.shape
    nx, nz, nc = (lax.axis_size("x"), lax.axis_size("z"), lax.axis_size("core"))
    experts = nx * nz * nc
    hit = routes[:, :, None] == jnp.arange(experts, dtype=jnp.int32)
    routed = hit.any(axis=1)
    gate_of = jnp.where(hit, gates[:, :, None], 0).sum(axis=1)
    below = jnp.tril(jnp.ones((rows, rows), jnp.bfloat16), -1)
    rank = jnp.dot(below, routed.astype(jnp.bfloat16), preferred_element_type=jnp.float32)
    rank = jnp.where(routed, rank, 200.0).astype(jnp.bfloat16)
    packed = jnp.concatenate([tokens, rank, gate_of.astype(jnp.bfloat16)], axis=1)
    held = lax.all_gather(packed, "z")
    mine = lax.axis_index("z")

    def at_z(a):
        a = a.reshape(nz, rows, nx, nz, nc)
        return lax.dynamic_index_in_dim(a, mine, 3, keepdims=False).reshape(nz, rows, nx * nc)

    rank_z = at_z(held[..., width : width + experts])
    gate_z = at_z(held[..., width + experts :])
    slots = jnp.arange(CAP, dtype=jnp.bfloat16)
    chosen = rank_z.transpose(2, 0, 1)[:, :, None, :] == slots[:, None]
    pick = chosen.astype(jnp.bfloat16)
    send = jnp.einsum(
        "dslt,stf->dslf", pick, held[..., :width], preferred_element_type=jnp.bfloat16
    )
    send = send.reshape(nx * nc, nz * CAP, width)
    recv = lax.all_to_all(send, ("x", "core"), split_axis=0, concat_axis=0, tiled=True)
    flat = recv.reshape(-1, width)
    gate_part = jnp.dot(flat, w_gate[0], preferred_element_type=jnp.float32)
    up_part = jnp.dot(flat, w_up[0], preferred_element_type=jnp.float32)
    hidden = (jax.nn.silu(gate_part) * up_part).astype(jnp.bfloat16)
    result = jnp.dot(hidden, w_down[0], preferred_element_type=jnp.float32).astype(jnp.bfloat16)
    back = lax.all_to_all(
        result.reshape(recv.shape), ("x", "core"), split_axis=0, concat_axis=0, tiled=True
    ).reshape(nx * nc, nz, CAP, width)
    mix = jnp.where(chosen, gate_z.transpose(2, 0, 1)[:, :, None, :], 0)
    part = jnp.einsum("dslt,dslf->stf", mix, back, preferred_element_type=jnp.float32)
    mixed = lax.psum_scatter(part.astype(jnp.bfloat16), "z", scatter_dimension=0, tiled=False)
    token_score = jnp.dot(mixed.astype(jnp.float32), score_head, precision=lax.Precision.HIGHEST)
    passage_score = token_score.reshape(-1, PASSAGE).sum(axis=1) / math.sqrt(PASSAGE)
    pair = jnp.stack([passage_score, doc_ids.astype(jnp.float32)], axis=1)
    pairs = lax.all_gather(pair, EP_DP, tiled=True)
    total = pairs.shape[0]
    docs = total // 4
    column = pairs[:, :1]
    member = pairs[:, 1:] == jnp.arange(docs, dtype=jnp.float32)[None, :]
    index = jnp.arange(total, dtype=jnp.int32)[:, None]
    max_score = jnp.where(member, column, -1e30).max(axis=0)
    sum_score = jnp.where(member, column, 0.0).sum(axis=0)
    first = jnp.where(member, index, total).min(axis=0)
    first_score = jnp.where(member & (index == first[None, :]), column, 0.0).sum(axis=0)
    return (mixed, jnp.stack([max_score, first_score, sum_score]))


def solution(mesh):
    finer = Mesh(mesh.devices.reshape(4, 8, 2, mesh.shape["dp"]), EP_DP)
    return jax.shard_map(
        shards,
        mesh=finer,
        in_specs=(
            P(EP_DP, None),
            P(EP_DP, None),
            P(EP_DP, None),
            P(EP, None, None),
            P(EP, None, None),
            P(EP, None, None),
            P(),
            P(EP_DP),
        ),
        out_specs=(P(EP_DP, None), P()),
        check_vma=False,
    )
```

profile of v0, /device:TPU:1, one launch (start us, length us, event | category | flops | bytes accessed | tf_op | source)
XLA Modules:
  0.0 412.3 jit_solution(16684683082836953582)
XLA Ops:
  7.2 0.0 copy-start
  7.2 0.0 all-gather.4.cloned.1.call-start
  7.2 0.9 fusion.14
  8.1 0.2 fusion.10
  8.3 0.1 copy.31
  8.5 0.7 fusion.19
  9.2 0.1 copy.32
  9.3 1.9 concatenate.3
  11.2 0.0 all-gather.4.cloned.1.call-update
  11.2 61.0 %all-gather.4.cloned.1.call-done = bf16[1024,2176]{1,0:T(8,128)(2,1)} async-done(((bf16[128,2176]{1,0:T(8,128)(2,1)}), bf16[1024,2176]{1,0:T(8,128)(2,1)}) %all-gather.4.cloned.1.call-update) | async-done | bytes 4456464 | tf_op jit(solution)/shard_map/all_gather | solution.py:26
  72.2 1.8 fusion.29
  74.0 1.1 copy.33
  75.1 0.8 copy.35
  75.9 0.7 constant_dynamic-slice_fusion
  76.6 4.0 fusion.3
  80.6 1.1 copy.37
  81.7 76.3 %all_to_all.10 = bf16[8,192,2048]{2,1,0:T(8,128)(2,1)S(1)} all-to-all(bf16[8,192,2048]{2,1,0:T(8,128)(2,1)S(1)} %bitcast.54), channel_id=1, replica_groups=mesh['x'=4,'z'=8,'core'=2,'dp'=4] {'x','core'}, dimensions={0} | all-to-all | bytes 12582912 | tf_op jit(solution)/shard_map/all_to_all | solution.py:42
  158.0 5.2 %fusion.8 = f32[1536,768]{1,0:T(8,128)S(1)} fusion(bf16[1536,2048]{1,0:T(8,128)(2,1)S(1)} %bitcast.56, bf16[1,2048,768]{2,1,0:T(8,128)(2,1)S(1)} %copy-done.2), kind=kOutput, calls=%fused_computation.10 | convolution fusion | flops 4831838208 | bytes 14155776 | tf_op jit(solution)/shard_map/dot_general | solution.py:44
  163.2 5.6 %multiply_convert_fusion = bf16[1536,768]{1,0:T(8,128)(2,1)S(1)} fusion(f32[1536,768]{1,0:T(8,128)S(1)} %fusion.8, bf16[1536,2048]{1,0:T(8,128)(2,1)S(1)} %bitcast.57, bf16[1,2048,768]{2,1,0:T(8,128)(2,1)S(1)} %copy-done.3), kind=kOutput, calls=%fused_computation.4 | convolution fusion | flops 4838916096 | bytes 16515072 | tf_op jit(solution)/shard_map/dot_general | solution.py:45
  168.9 7.0 %convolution_convert_fusion = bf16[1536,2048]{1,0:T(8,128)(2,1)} fusion(bf16[1536,768]{1,0:T(8,128)(2,1)S(1)} %multiply_convert_fusion, bf16[1,768,2048]{2,1,0:T(8,128)(2,1)S(1)} %copy-done), kind=kOutput, calls=%fused_computation.1 | convolution fusion | flops 4834983936 | bytes 11796480 | tf_op jit(solution)/shard_map/dot_general | solution.py:47
  175.9 5.7 %all-to-all-start.1 = ((bf16[8,192,2048]{2,1,0:T(8,128)(2,1)}), bf16[8,192,2048]{2,1,0:T(8,128)(2,1)}, u32[]{:S(2)}, u32[]{:S(2)}) async-start(bf16[8,192,2048]{2,1,0:T(8,128)(2,1)} %bitcast.55), calls=%async_computation.1 | async-start | bytes 12582912 | tf_op jit(solution)/shard_map/all_to_all | solution.py:48
  181.6 71.3 %all-to-all-done.1 = bf16[8,192,2048]{2,1,0:T(8,128)(2,1)} async-done(((bf16[8,192,2048]{2,1,0:T(8,128)(2,1)}), bf16[8,192,2048]{2,1,0:T(8,128)(2,1)}, u32[]{:S(2)}, u32[]{:S(2)}) %all-to-all-start.1) | async-done | bytes 6291488 | tf_op jit(solution)/shard_map/all_to_all | solution.py:48
  252.8 6.1 %bitcast_convert_fusion = bf16[8,128,2048]{2,1,0:T(8,128)(2,1)} fusion(bf16[8,8,24,2048]{3,2,1,0:T(8,128)(2,1)} %bitcast.16, bf16[8,8,128]{2,0,1:T(8,128)(2,1)S(1)} %copy.36, bf16[8,8,128]{2,0,1:T(8,128)(2,1)S(1)} %copy.34), kind=kOutput, calls=%fused_computation | convolution fusion | flops 808189952 | bytes 10518528 | tf_op jit(solution)/shard_map/dslt,dslf->stf/dot_general | solution.py:52
  259.0 0.0 reduce-scatter.2.cloned.1.call-update
  259.6 51.8 %reduce-scatter.2.cloned.1.call-done = bf16[1,128,2048]{2,1,0:T(8,128)(2,1)} async-done(((bf16[8,128,2048]{2,1,0:T(8,128)(2,1)}), bf16[1,128,2048]{2,1,0:T(8,128)(2,1)}) %reduce-scatter.2.cloned.1.call-update) | async-done | bytes 524304 | tf_op jit(solution)/shard_map/reduce_scatter | solution.py:53
  311.5 2.2 fusion.11
  314.4 0.1 maximum_bitcast_fusion
  314.5 89.8 %all-gather.1 = f32[256,1,2]{2,1,0:T(1,128)S(1)} all-gather(f32[1,1,2]{2,1,0:T(1,128)S(1)} %maximum_bitcast_fusion), channel_id=1, replica_groups=mesh['x'=4,'z'=8,'core'=2,'dp'=4] {'x','z','core','dp'}, dimensions={0}, use_global_device_ids=true | all-gather | bytes 2056 | tf_op jit(solution)/shard_map/all_gather | solution.py:57
  404.3 0.2 slice_reduce_fusion.1
  404.5 0.1 select_reduce_fusion.2
  404.7 0.2 select_reduce_fusion.3
  404.8 0.6 pad_maximum_fusion
  (11 shorter events, 0.0 us)
Async XLA Ops:
  7.2 161.7 %copy-start = (bf16[1,768,2048]{2,1,0:T(8,128)(2,1)S(1)}, bf16[1,768,2048]{2,1,0:T(8,128)(2,1)}, u32[]{:S(2)}) copy-start(bf16[1,768,2048]{2,1,0:T(8,128)(2,1)} %param.13) | copy-start | bytes 9437188
  7.2 65.0 %all-gather.4.cloned.1.call-start = ((), (), s32[]{:S(2)}) async-start(), calls=%async_computation.4 | async-start | bytes 5013504 | tf_op jit(solution)/shard_map/all_gather | solution.py:26
  81.7 76.3 %copy-start.2 = (bf16[1,2048,768]{2,1,0:T(8,128)(2,1)S(1)}, bf16[1,2048,768]{2,1,0:T(8,128)(2,1)}, u32[]{:S(2)}) copy-start(bf16[1,2048,768]{2,1,0:T(8,128)(2,1)} %param.11) | copy-start | bytes 9437188
  158.0 5.2 %copy-start.3 = (bf16[1,2048,768]{2,1,0:T(8,128)(2,1)S(1)}, bf16[1,2048,768]{2,1,0:T(8,128)(2,1)}, u32[]{:S(2)}) copy-start(bf16[1,2048,768]{2,1,0:T(8,128)(2,1)} %param.12) | copy-start | bytes 9437188
  175.9 76.9 %all-to-all-start.1 = ((bf16[8,192,2048]{2,1,0:T(8,128)(2,1)}), bf16[8,192,2048]{2,1,0:T(8,128)(2,1)}, u32[]{:S(2)}, u32[]{:S(2)}) async-start(bf16[8,192,2048]{2,1,0:T(8,128)(2,1)} %bitcast.55), calls=%async_computation.1 | async-start | bytes 12582912 | tf_op jit(solution)/shard_map/all_to_all | solution.py:48
  181.6 129.9 %reduce-scatter.2.cloned.1.call-start = ((), (), s32[]{:S(2)}) async-start(), calls=%async_computation.3 | async-start | bytes 4718592 | tf_op jit(solution)/shard_map/reduce_scatter | solution.py:53
  252.8 58.6 %copy-start.1 = (f32[2048]{0:T(1024)S(1)}, f32[2048]{0:T(1024)}, u32[]{:S(2)}) copy-start(f32[2048]{0:T(1024)} %param.14) | copy-start | bytes 24580
Sparse Core Ops, SparseCore 0:
  11.3 60.8 all-gather.3
  259.1 52.2 reduce-scatter.1
where the time goes:
time: 413 us; the launch traced here: 412 us
  waiting for transfers between devices  184 us (45%)
  blocking collectives  166 us (40%)
  matrix products  30.4 us (7%)
  between operations  15.5 us (4%)
  local copies, waits for them, and re-layouts  7.92 us (2%)
  starting transfers between devices  5.71 us (1%)
    all_gather x1, blocking collectives, shards(): pairs = lax.all_gather(pair, EP_DP, tiled=True)  89.8 us
    all_to_all x1, blocking collectives, shards(): lax.all_to_all(send, ('x', 'core'), split_axis=0, concat_axis=0, tiled=True)  76.3 us
    all_to_all x1, waiting for transfers between devices, shards(): lax.all_to_all(result.reshape(recv.shape), ('x', 'core'), split_axis=0, c...  71.3 us
    all_gather x1, waiting for transfers between devices, shards(): held = lax.all_gather(packed, 'z')  61 us
    reduce_scatter x1, waiting for transfers between devices, shards(): lax.psum_scatter(part.astype(jnp.bfloat16), 'z', scatter_dimension=0, til...  51.8 us
  transfers between devices with their start and end apart: 3, of which 3 were waited for; matrix products, arithmetic and copies ran while one was open for 0% of the time, Pallas kernels for 0%

commit v1 on v0

--- a/solution.py
+++ b/solution.py
@@ -54,7 +54,9 @@
     token_score = jnp.dot(mixed.astype(jnp.float32), score_head, precision=lax.Precision.HIGHEST)
     passage_score = token_score.reshape(-1, PASSAGE).sum(axis=1) / math.sqrt(PASSAGE)
     pair = jnp.stack([passage_score, doc_ids.astype(jnp.float32)], axis=1)
-    pairs = lax.all_gather(pair, EP_DP, tiled=True)
+    pairs = jnp.concatenate(
+        lax.all_to_all(jnp.stack([pair] * lax.axis_size(EP_DP)), EP_DP, 0, 0), axis=0
+    )
     total = pairs.shape[0]
     docs = total // 4
     column = pairs[:, :1]

time: 413 us -> 346 us (0.84)
  blocking collectives: 166 us -> 99.4 us
    all_gather x1 -> x0, blocking collectives: 89.8 us -> none  [shards(): pairs = lax.all_gather(pair, EP_DP, tiled=True)]
    all_to_all x0 -> x1, blocking collectives: none -> 23.2 us  [shards(): lax.all_to_all(jnp.stack([pair] * lax.axis_size(EP_DP)), EP_DP, 0, 0)]
where the time goes in v1:
time: 346 us
  waiting for transfers between devices  184 us (53%)
  blocking collectives  99.4 us (29%)
  matrix products  30.4 us (9%)
  between operations  15.5 us (4%)
  local copies, waits for them, and re-layouts  7.99 us (2%)
  starting transfers between devices  5.71 us (2%)
    all_to_all x1, blocking collectives, shards(): lax.all_to_all(send, ('x', 'core'), split_axis=0, concat_axis=0, tiled=True)  76.3 us
    all_to_all x1, waiting for transfers between devices, shards(): lax.all_to_all(result.reshape(recv.shape), ('x', 'core'), split_axis=0, c...  71.3 us
    all_gather x1, waiting for transfers between devices, shards(): held = lax.all_gather(packed, 'z')  61 us
    reduce_scatter x1, waiting for transfers between devices, shards(): lax.psum_scatter(part.astype(jnp.bfloat16), 'z', scatter_dimension=0, til...  51.8 us
    all_to_all x1, blocking collectives, shards(): lax.all_to_all(jnp.stack([pair] * lax.axis_size(EP_DP)), EP_DP, 0, 0)  23.2 us
    dot_general x1, matrix products, shards(): jnp.dot(hidden, w_down[0], preferred_element_type=jnp.float32)  7.02 us
  transfers between devices with their start and end apart: 3, of which 3 were waited for; matrix products, arithmetic and copies ran while one was open for 0% of the time, Pallas kernels for 0%

profile of v1, /device:TPU:1, one launch (start us, length us, event | category | flops | bytes accessed | tf_op | source)
XLA Modules:
  0.0 345.7 jit_solution(7939566150697138938)
XLA Ops:
  7.2 0.0 all-gather.3.cloned.1.call-start
  7.2 0.9 fusion.14
  8.1 0.2 fusion.10
  8.3 0.1 copy.31
  8.5 0.7 fusion.19
  9.2 0.1 copy.32
  9.3 1.9 concatenate.3
  11.2 0.0 all-gather.3.cloned.1.call-update
  11.2 61.0 %all-gather.3.cloned.1.call-done = bf16[1024,2176]{1,0:T(8,128)(2,1)} async-done(((bf16[128,2176]{1,0:T(8,128)(2,1)}), bf16[1024,2176]{1,0:T(8,128)(2,1)}) %all-gather.3.cloned.1.call-update) | async-done | bytes 4456464 | tf_op jit(solution)/shard_map/all_gather | solution.py:26
  72.2 1.8 fusion.29
  74.0 1.1 copy.33
  75.1 0.8 copy.35
  75.9 0.7 constant_dynamic-slice_fusion
  76.6 4.0 %fusion.3 = bf16[8,8,24,2048]{3,2,0,1:T(8,128)(2,1)S(1)} fusion(bf16[8,128,2176]{2,1,0:T(8,128)(2,1)} %bitcast.66, bf16[8,8,128]{2,0,1:T(8,128)(2,1)S(1)} %copy.34), kind=kOutput, calls=%fused_computation.7 | convolution fusion | flops 805896192 | bytes 10502144 | tf_op jit(solution)/shard_map/dslt,stf->dslf/dot_general | solution.py:38
  80.6 1.1 copy.37
  81.7 76.3 %all_to_all.15 = bf16[8,192,2048]{2,1,0:T(8,128)(2,1)S(1)} all-to-all(bf16[8,192,2048]{2,1,0:T(8,128)(2,1)S(1)} %bitcast.54), channel_id=1, replica_groups=mesh['x'=4,'z'=8,'core'=2,'dp'=4] {'x','core'}, dimensions={0} | all-to-all | bytes 12582912 | tf_op jit(solution)/shard_map/all_to_all | solution.py:42
  158.0 5.2 %fusion.8 = f32[1536,768]{1,0:T(8,128)S(1)} fusion(bf16[1536,2048]{1,0:T(8,128)(2,1)S(1)} %bitcast.56, bf16[1,2048,768]{2,1,0:T(8,128)(2,1)S(1)} %copy-done.2), kind=kOutput, calls=%fused_computation.10 | convolution fusion | flops 4831838208 | bytes 14155776 | tf_op jit(solution)/shard_map/dot_general | solution.py:44
  163.2 5.6 %multiply_convert_fusion = bf16[1536,768]{1,0:T(8,128)(2,1)S(1)} fusion(f32[1536,768]{1,0:T(8,128)S(1)} %fusion.8, bf16[1536,2048]{1,0:T(8,128)(2,1)S(1)} %bitcast.57, bf16[1,2048,768]{2,1,0:T(8,128)(2,1)S(1)} %copy-done.3), kind=kOutput, calls=%fused_computation.4 | convolution fusion | flops 4838916096 | bytes 16515072 | tf_op jit(solution)/shard_map/dot_general | solution.py:45
  168.9 7.0 %convolution_convert_fusion = bf16[1536,2048]{1,0:T(8,128)(2,1)} fusion(bf16[1536,768]{1,0:T(8,128)(2,1)S(1)} %multiply_convert_fusion, bf16[1,768,2048]{2,1,0:T(8,128)(2,1)S(1)} %copy-done), kind=kOutput, calls=%fused_computation.1 | convolution fusion | flops 4834983936 | bytes 11796480 | tf_op jit(solution)/shard_map/dot_general | solution.py:47
  175.9 5.7 %all-to-all-start.1 = ((bf16[8,192,2048]{2,1,0:T(8,128)(2,1)}), bf16[8,192,2048]{2,1,0:T(8,128)(2,1)}, u32[]{:S(2)}, u32[]{:S(2)}) async-start(bf16[8,192,2048]{2,1,0:T(8,128)(2,1)} %bitcast.55), calls=%async_computation.1 | async-start | bytes 12582912 | tf_op jit(solution)/shard_map/all_to_all | solution.py:48
  181.6 71.3 %all-to-all-done.1 = bf16[8,192,2048]{2,1,0:T(8,128)(2,1)} async-done(((bf16[8,192,2048]{2,1,0:T(8,128)(2,1)}), bf16[8,192,2048]{2,1,0:T(8,128)(2,1)}, u32[]{:S(2)}, u32[]{:S(2)}) %all-to-all-start.1) | async-done | bytes 6291488 | tf_op jit(solution)/shard_map/all_to_all | solution.py:48
  252.8 6.1 %bitcast_convert_fusion = bf16[8,128,2048]{2,1,0:T(8,128)(2,1)} fusion(bf16[8,8,24,2048]{3,2,1,0:T(8,128)(2,1)} %bitcast.16, bf16[8,8,128]{2,0,1:T(8,128)(2,1)S(1)} %copy.36, bf16[8,8,128]{2,0,1:T(8,128)(2,1)S(1)} %copy.34), kind=kOutput, calls=%fused_computation | convolution fusion | flops 808189952 | bytes 10518528 | tf_op jit(solution)/shard_map/dslt,dslf->stf/dot_general | solution.py:52
  259.0 0.0 reduce-scatter.2.cloned.1.call-update
  259.6 51.8 %reduce-scatter.2.cloned.1.call-done = bf16[1,128,2048]{2,1,0:T(8,128)(2,1)} async-done(((bf16[8,128,2048]{2,1,0:T(8,128)(2,1)}), bf16[1,128,2048]{2,1,0:T(8,128)(2,1)}) %reduce-scatter.2.cloned.1.call-update) | async-done | bytes 524304 | tf_op jit(solution)/shard_map/reduce_scatter | solution.py:53
  311.5 2.2 fusion.11
  314.4 0.1 maximum_bitcast_fusion
  314.5 0.1 stack.22
  314.6 23.2 %all_to_all.16 = f32[256,1,2]{2,1,0:T(1,128)S(1)} all-to-all(f32[256,1,2]{2,1,0:T(1,128)S(1)} %stack.22), channel_id=1, replica_groups=mesh['x'=4,'z'=8,'core'=2,'dp'=4] {'x','z','core','dp'}, dimensions={0} | all-to-all | bytes 4096 | tf_op jit(solution)/shard_map/all_to_all | solution.py:58
  337.7 0.2 slice_reduce_fusion.1
  338.0 0.1 select_reduce_fusion.2
  338.1 0.2 select_reduce_fusion.3
  338.3 0.6 pad_maximum_fusion
  (12 shorter events, 0.0 us)
Async XLA Ops:
  7.2 161.7 %copy-start = (bf16[1,768,2048]{2,1,0:T(8,128)(2,1)S(1)}, bf16[1,768,2048]{2,1,0:T(8,128)(2,1)}, u32[]{:S(2)}) copy-start(bf16[1,768,2048]{2,1,0:T(8,128)(2,1)} %param.13) | copy-start | bytes 9437188
  7.2 65.0 %all-gather.3.cloned.1.call-start = ((), (), s32[]{:S(2)}) async-start(), calls=%async_computation.5 | async-start | bytes 5013504 | tf_op jit(solution)/shard_map/all_gather | solution.py:26
  81.7 76.3 %copy-start.2 = (bf16[1,2048,768]{2,1,0:T(8,128)(2,1)S(1)}, bf16[1,2048,768]{2,1,0:T(8,128)(2,1)}, u32[]{:S(2)}) copy-start(bf16[1,2048,768]{2,1,0:T(8,128)(2,1)} %param.11) | copy-start | bytes 9437188
  158.0 5.2 %copy-start.3 = (bf16[1,2048,768]{2,1,0:T(8,128)(2,1)S(1)}, bf16[1,2048,768]{2,1,0:T(8,128)(2,1)}, u32[]{:S(2)}) copy-start(bf16[1,2048,768]{2,1,0:T(8,128)(2,1)} %param.12) | copy-start | bytes 9437188
  175.9 76.9 %all-to-all-start.1 = ((bf16[8,192,2048]{2,1,0:T(8,128)(2,1)}), bf16[8,192,2048]{2,1,0:T(8,128)(2,1)}, u32[]{:S(2)}, u32[]{:S(2)}) async-start(bf16[8,192,2048]{2,1,0:T(8,128)(2,1)} %bitcast.55), calls=%async_computation.1 | async-start | bytes 12582912 | tf_op jit(solution)/shard_map/all_to_all | solution.py:48
  181.6 129.9 %reduce-scatter.2.cloned.1.call-start = ((), (), s32[]{:S(2)}) async-start(), calls=%async_computation.4 | async-start | bytes 4718592 | tf_op jit(solution)/shard_map/reduce_scatter | solution.py:53
  252.8 58.6 %copy-start.1 = (f32[2048]{0:T(1024)S(1)}, f32[2048]{0:T(1024)}, u32[]{:S(2)}) copy-start(f32[2048]{0:T(1024)} %param.14) | copy-start | bytes 24580
Sparse Core Ops, SparseCore 0:
  11.3 60.8 all-gather.2
  259.1 52.2 reduce-scatter.1
